TPU v7x, 32 devices: a whole 2x2x4 slice. The times are simulated.
32 devices in a mesh: dp: 8 (over z, x), rep: 4 (over y, core).
Axes of the slice: x: 2, y: 2, z: 4, core: 2. Of those that a mesh axis runs over, the one named last changes fastest.
Arguments:
- tokens: bfloat16 [65536, 1280], P(('dp', 'rep')), may hold values from -6 to 6
- sketch_map: bfloat16 [65536, 128], P(('dp', 'rep')), may hold values from -0.125 to 0.125
- test_matrix: bfloat16 [4, 1024, 128], P('rep'), may hold values from -0.09375 to 0.09375
Outputs:
- basis: float32 [1280, 128], P('dp')
- factor: float32 [128, 128], replicated
All inputs are finite; a program needn't handle non-finite values.
Results may differ from a plain program's by a relative error of at most 0.0051.
Values may be sent and summed in bfloat16 or wider, within the bound.
A program may use at most 64 MiB of HBM per device.

v0:
```python
import jax
import jax.numpy as jnp
from jax import lax
from jax.sharding import PartitionSpec as P

ITERS = 2


def whole_factor(matrix):
    gram = jnp.dot(
        matrix.T, matrix, precision=lax.Precision.HIGHEST, preferred_element_type=jnp.float32
    )
    lower = jnp.linalg.cholesky(gram)
    return (jax.scipy.linalg.solve_triangular(lower, matrix.T, lower=True).T, lower.T)


def body(tokens, sketch_map, test_matrix):
    width = tokens.shape[1]
    strip = width // lax.axis_size("dp")
    total_tokens = tokens.shape[0] * lax.axis_size("dp") * lax.axis_size("rep")
    sketch = lax.dot_general(
        sketch_map, tokens, (((0,), (0,)), ((), ())), preferred_element_type=jnp.float32
    ).astype(jnp.bfloat16)
    merged = lax.all_to_all(sketch, "dp", split_axis=1, concat_axis=0, tiled=True)
    local_start = lax.dot_general(
        merged, test_matrix[0], (((0,), (0,)), ((), ())), preferred_element_type=jnp.float32
    )
    start = lax.psum(local_start, "rep")
    gathered = lax.all_gather(start, "dp", axis=0, tiled=True)
    current, factor = whole_factor(gathered)
    for step in range(ITERS):
        rounded = current.astype(jnp.bfloat16)
        projected = jnp.dot(tokens, rounded, preferred_element_type=jnp.float32).astype(
            jnp.bfloat16
        )
        local_sum = lax.dot_general(
            tokens, projected, (((0,), (0,)), ((), ())), preferred_element_type=jnp.float32
        )
        summed = lax.psum(local_sum, ("dp", "rep"))
        current, factor = whole_factor(summed / total_tokens)
    owned = lax.dynamic_slice_in_dim(current, lax.axis_index("dp") * strip, strip, 0)
    return (owned, factor)


def solution(mesh):
    return jax.shard_map(
        body,
        mesh=mesh,
        in_specs=(P(("dp", "rep"), None), P(("dp", "rep"), None), P("rep", None, None)),
        out_specs=(P("dp", None), P()),
        check_vma=False,
    )
```

profile of v0, /device:TPU:0, one launch (start us, length us, event | category | flops | bytes accessed | tf_op | source)
XLA Modules:
  0.0 453.5 jit_solution(7895339741333896489)
XLA Ops:
  7.2 1.0 copy-done
  8.2 3.4 convolution_convert_fusion.4
  11.6 0.2 copy.9
  11.8 18.0 %all_to_all.19 = bf16[128,8,160]{0,2,1:T(8,128)(2,1)S(1)} all-to-all(bf16[128,8,160]{0,2,1:T(8,128)(2,1)S(1)} %bitcast.66), channel_id=1, replica_groups=mesh['dp'=8,'rep'=4] {'dp'}, dimensions={1} | all-to-all | bytes 655360 | tf_op jit(solution)/shard_map/all_to_all | solution.py:24
  29.8 0.9 fusion.10
  30.7 28.8 %all-reduce.4.cloned.1.call-done = f32[160,128]{1,0:T(8,128)} async-done(((f32[160,128]{1,0:T(8,128)}), f32[160,128]{1,0:T(8,128)}) %all-reduce.4.cloned.1.call-update) | async-done | bytes 81936 | tf_op jit(solution)/shard_map/psum | solution.py:28
  59.5 32.0 %all_gather.3 = f32[1280,128]{1,0:T(8,128)S(1)} all-gather(f32[160,128]{1,0:T(8,128)} %all-reduce.4.cloned.1.call-done), channel_id=1, replica_groups=mesh['dp'=8,'rep'=4] {'dp'}, dimensions={0}, use_global_device_ids=true | all-gather | bytes 737280 | tf_op jit(solution)/shard_map/all_gather | solution.py:29
  91.5 1.2 fusion.36
  92.8 11.7 %cholesky.59 = f32[128,128]{1,0:T(8,128)S(1)} custom-call(f32[128,128]{1,0:T(8,128)S(1)} %fusion.25), custom_call_target="Cholesky" | custom-call | tf_op jit(solution)/shard_map/jit(cholesky)/cholesky | solution.py:13
  104.6 0.6 compare_reduce_fusion.2
  105.2 0.7 fusion.18
  105.9 9.8 %custom-call.7 = f32[1,128,128]{1,2,0:T(8,128)S(1)} custom-call(f32[1,128,128]{2,1,0:T(8,128)S(1)} %fusion.18), custom_call_target="InvertDiagBlocksLowerTriangular" | custom-call | tf_op jit(solution)/shard_map/jit(_solve_triangular)/triangular_solve | solution.py:14
  115.7 0.8 convolution_convert_fusion.3
  116.5 7.5 %convolution_bitcast_fusion.1 = f32[1280,128]{0,1:T(8,128)} fusion(bf16[2048,1280]{1,0:T(8,128)(2,1)} %param.6, bf16[128,1280]{1,0:T(8,128)(2,1)S(1)} %convolution_convert_fusion.3), kind=kOutput, calls=%fused_computation.1 | convolution fusion | flops 1342439424 | bytes 6225920 | tf_op jit(solution)/shard_map/dot_general | solution.py:36
  124.0 0.2 all-reduce.8.cloned.1.call-start
  124.2 130.7 %all-reduce.6.cloned.1.call-done = f32[1280,128]{0,1:T(8,128)} async-done(((f32[1280,128]{0,1:T(8,128)}), f32[1280,128]{0,1:T(8,128)}) %all-reduce.6.cloned.1.call-update) | async-done | bytes 655376 | tf_op jit(solution)/shard_map/psum | solution.py:39
  255.0 2.0 fusion.8
  257.1 11.7 %cholesky.70 = f32[128,128]{1,0:T(8,128)S(1)} custom-call(f32[128,128]{1,0:T(8,128)S(1)} %fusion.23), custom_call_target="Cholesky" | custom-call | tf_op jit(solution)/shard_map/jit(cholesky)/cholesky | solution.py:13
  268.9 0.6 compare_reduce_fusion.1
  269.5 0.7 fusion.19
  270.2 9.8 %custom-call.8 = f32[1,128,128]{1,2,0:T(8,128)S(1)} custom-call(f32[1,128,128]{2,1,0:T(8,128)S(1)} %fusion.19), custom_call_target="InvertDiagBlocksLowerTriangular" | custom-call | tf_op jit(solution)/shard_map/jit(_solve_triangular)/triangular_solve | solution.py:14
  280.0 1.8 convolution_convert_fusion.1
  281.8 7.5 %convolution_bitcast_fusion = f32[1280,128]{0,1:T(8,128)} fusion(bf16[2048,1280]{1,0:T(8,128)(2,1)} %param.6, bf16[128,1280]{1,0:T(8,128)(2,1)S(1)} %convolution_convert_fusion.1), kind=kOutput, calls=%fused_computation | convolution fusion | flops 1342439424 | bytes 6225920 | tf_op jit(solution)/shard_map/dot_general | solution.py:36
  289.3 128.8 %all-reduce.8.cloned.1.call-done = f32[1280,128]{0,1:T(8,128)} async-done(((f32[1280,128]{0,1:T(8,128)}), f32[1280,128]{0,1:T(8,128)}) %all-reduce.8.cloned.1.call-update) | async-done | bytes 655376 | tf_op jit(solution)/shard_map/psum | solution.py:39
  418.1 2.0 fusion.5
  420.2 11.9 %cholesky.81 = f32[128,128]{1,0:T(8,128)S(1)} custom-call(f32[128,128]{1,0:T(8,128)S(1)} %fusion.21), custom_call_target="Cholesky" | custom-call | tf_op jit(solution)/shard_map/jit(cholesky)/cholesky | solution.py:13
  432.2 0.6 compare_reduce_fusion
  432.8 0.7 fusion.31
  433.5 9.8 %custom-call.9 = f32[1,128,128]{1,2,0:T(8,128)S(1)} custom-call(f32[1,128,128]{2,1,0:T(8,128)S(1)} %get-tuple-element.9), custom_call_target="InvertDiagBlocksLowerTriangular" | custom-call | tf_op jit(solution)/shard_map/jit(_solve_triangular)/triangular_solve | solution.py:14
  443.3 0.7 copy.14
  444.0 2.3 fusion
  446.3 0.6 dynamic-slice_bitcast_fusion
  (17 shorter events, 0.6 us)
Async XLA Ops:
  7.2 1.0 copy-start
  7.2 22.6 %copy-start.1 = (bf16[1,1024,128]{2,1,0:T(8,128)(2,1)S(1)}, bf16[1,1024,128]{2,1,0:T(8,128)(2,1)}, u32[]{:S(2)}) copy-start(bf16[1,1024,128]{2,1,0:T(8,128)(2,1)} %param.8) | copy-start | bytes 786436
  7.2 52.3 %all-reduce.4.cloned.1.call-start = ((), (), s32[]{:S(2)}) async-start(), calls=%async_computation.1 | async-start | bytes 163840 | tf_op jit(solution)/shard_map/psum | solution.py:28
  30.7 224.3 %all-reduce.6.cloned.1.call-start = ((), (), s32[]{:S(2)}) async-start(), calls=%async_computation.2 | async-start | bytes 1310720 | tf_op jit(solution)/shard_map/psum | solution.py:39
  124.0 294.1 %all-reduce.8.cloned.1.call-start = ((), (), s32[]{:S(2)}) async-start(), calls=%async_computation.3 | async-start | bytes 1310720 | tf_op jit(solution)/shard_map/psum | solution.py:39
Sparse Core Ops, SparseCore 0:
  30.8 28.6 all-reduce.3
  124.1 130.8 all-reduce.5
  289.5 128.6 all-reduce.7
where the time goes:
time: 454 us
  waiting for transfers between devices  288 us (63%)
  other arithmetic  68.8 us (15%)
  blocking collectives  50 us (11%)
  matrix products  29.3 us (6%)
  between operations  13.9 us (3%)
    psum x2, waiting for transfers between devices, body(): summed = lax.psum(local_sum, ('dp', 'rep'))  260 us
    another operation x9, other arithmetic, whole_factor(): lower = jnp.linalg.cholesky(gram)  37.4 us
    all_gather x1, blocking collectives, body(): gathered = lax.all_gather(start, 'dp', axis=0, tiled=True)  32 us
    another operation x5, other arithmetic, whole_factor(): jax.scipy.linalg.solve_triangular(lower, matrix.T, lower=True)  30.7 us
    psum x1, waiting for transfers between devices, body(): start = lax.psum(local_start, 'rep')  28.8 us
    all_to_all x1, blocking collectives, body(): lax.all_to_all(sketch, 'dp', split_axis=1, concat_axis=0, tiled=True)  18 us
    dot_general x2, matrix products, body(): lax.dot_general(tokens, projected, (((0,), (0,)), ((), ())), preferred_el...  15 us
  transfers between devices with their start and end apart: 3, of which 3 were waited for; matrix products, arithmetic and copies ran while one was open for 0% of the time, Pallas kernels for 0%

commit v1 on v0

--- a/solution.py
+++ b/solution.py
@@ -4,6 +4,11 @@
 from jax.sharding import PartitionSpec as P
 
 ITERS = 2
+
+
+def gather_and_add(block, mesh_axis):
+    parts = lax.all_gather(block, mesh_axis)
+    return jnp.sum(parts, axis=0)
 
 
 def whole_factor(matrix):
@@ -25,7 +30,7 @@
     local_start = lax.dot_general(
         merged, test_matrix[0], (((0,), (0,)), ((), ())), preferred_element_type=jnp.float32
     )
-    start = lax.psum(local_start, "rep")
+    start = gather_and_add(local_start, "rep")
     gathered = lax.all_gather(start, "dp", axis=0, tiled=True)
     current, factor = whole_factor(gathered)
     for step in range(ITERS):

time: 454 us -> 428 us (0.943)
  waiting for transfers between devices: 288 us -> 256 us
  blocking collectives: 50 us -> 55.9 us
    psum x1 -> x0, waiting for transfers between devices: 28.8 us -> none  [body(): start = lax.psum(local_start, 'rep')]
    all_gather x0 -> x1, blocking collectives: none -> 6.13 us  [gather_and_add(): parts = lax.all_gather(block, mesh_axis)]
  transfers between devices with their start and end apart: 3 -> 2, of which waited for: 3 -> 2; matrix products, arithmetic and copies ran while one was open for 0% -> 0% of each run, Pallas kernels for 0% -> 0%
where the time goes in v1:
time: 428 us; the launch traced here: 427 us
  waiting for transfers between devices  256 us (60%)
  other arithmetic  68.8 us (16%)
  blocking collectives  55.9 us (13%)
  matrix products  28.7 us (7%)
  between operations  14.2 us (3%)
    psum x2, waiting for transfers between devices, body(): summed = lax.psum(local_sum, ('dp', 'rep'))  256 us
    another operation x9, other arithmetic, whole_factor(): lower = jnp.linalg.cholesky(gram)  37.4 us
    all_gather x1, blocking collectives, body(): gathered = lax.all_gather(start, 'dp', axis=0, tiled=True)  31.7 us
    another operation x5, other arithmetic, whole_factor(): jax.scipy.linalg.solve_triangular(lower, matrix.T, lower=True)  30.7 us
    all_to_all x1, blocking collectives, body(): lax.all_to_all(sketch, 'dp', split_axis=1, concat_axis=0, tiled=True)  18 us
    dot_general x2, matrix products, body(): lax.dot_general(tokens, projected, (((0,), (0,)), ((), ())), preferred_el...  15 us
  transfers between devices with their start and end apart: 2, of which 2 were waited for; matrix products, arithmetic and copies ran while one was open for 0% of the time, Pallas kernels for 0%

profile of v1, /device:TPU:0, one launch (start us, length us, event | category | flops | bytes accessed | tf_op | source)
XLA Modules:
  0.0 427.2 jit_solution(162333316408541677)
XLA Ops:
  7.2 1.0 copy-done
  8.2 3.4 convolution_convert_fusion.4
  11.6 0.2 copy.9
  11.8 18.0 %all_to_all.19 = bf16[128,8,160]{0,2,1:T(8,128)(2,1)S(1)} all-to-all(bf16[128,8,160]{0,2,1:T(8,128)(2,1)S(1)} %bitcast.68), channel_id=1, replica_groups=mesh['dp'=8,'rep'=4] {'dp'}, dimensions={1} | all-to-all | bytes 655360 | tf_op jit(solution)/shard_map/all_to_all | solution.py:29
  29.8 0.2 fusion.10
  30.0 6.1 %all-gather = f32[640,128]{1,0:T(8,128)S(1)} all-gather(f32[160,128]{1,0:T(8,128)S(1)} %fusion.10), channel_id=2, replica_groups=mesh['dp'=8,'rep'=4] {'rep'}, dimensions={0}, use_global_device_ids=true | all-gather | bytes 409600 | tf_op jit(solution)/shard_map/all_gather | solution.py:10
  36.2 31.7 %all_gather.11 = f32[1280,128]{1,0:T(8,128)S(1)} all-gather(f32[160,128]{1,0:T(8,128)S(1)} %reduce_sum.9), channel_id=1, replica_groups=mesh['dp'=8,'rep'=4] {'dp'}, dimensions={0}, use_global_device_ids=true | all-gather | bytes 737280 | tf_op jit(solution)/shard_map/all_gather | solution.py:34
  67.9 1.2 fusion.36
  69.3 11.7 %cholesky.59 = f32[128,128]{1,0:T(8,128)S(1)} custom-call(f32[128,128]{1,0:T(8,128)S(1)} %fusion.25), custom_call_target="Cholesky" | custom-call | tf_op jit(solution)/shard_map/jit(cholesky)/cholesky | solution.py:18
  81.0 0.6 compare_reduce_fusion.2
  81.7 0.7 fusion.18
  82.3 9.8 %custom-call.7 = f32[1,128,128]{1,2,0:T(8,128)S(1)} custom-call(f32[1,128,128]{2,1,0:T(8,128)S(1)} %fusion.18), custom_call_target="InvertDiagBlocksLowerTriangular" | custom-call | tf_op jit(solution)/shard_map/jit(_solve_triangular)/triangular_solve | solution.py:19
  92.1 0.8 convolution_convert_fusion.3
  92.9 7.5 %convolution_bitcast_fusion.1 = f32[1280,128]{0,1:T(8,128)} fusion(bf16[2048,1280]{1,0:T(8,128)(2,1)} %param.6, bf16[128,1280]{1,0:T(8,128)(2,1)S(1)} %convolution_convert_fusion.3), kind=kOutput, calls=%fused_computation.1 | convolution fusion | flops 1342439424 | bytes 6225920 | tf_op jit(solution)/shard_map/dot_general | solution.py:41
  100.4 0.2 all-reduce.5.cloned.1.call-start
  100.7 127.7 %all-reduce.3.cloned.1.call-done = f32[1280,128]{0,1:T(8,128)} async-done(((f32[1280,128]{0,1:T(8,128)}), f32[1280,128]{0,1:T(8,128)}) %all-reduce.3.cloned.1.call-update) | async-done | bytes 655376 | tf_op jit(solution)/shard_map/psum | solution.py:44
  228.3 2.0 fusion.8
  230.4 11.7 %cholesky.70 = f32[128,128]{1,0:T(8,128)S(1)} custom-call(f32[128,128]{1,0:T(8,128)S(1)} %fusion.23), custom_call_target="Cholesky" | custom-call | tf_op jit(solution)/shard_map/jit(cholesky)/cholesky | solution.py:18
  242.2 0.6 compare_reduce_fusion.1
  242.8 0.7 fusion.19
  243.5 9.8 %custom-call.8 = f32[1,128,128]{1,2,0:T(8,128)S(1)} custom-call(f32[1,128,128]{2,1,0:T(8,128)S(1)} %fusion.19), custom_call_target="InvertDiagBlocksLowerTriangular" | custom-call | tf_op jit(solution)/shard_map/jit(_solve_triangular)/triangular_solve | solution.py:19
  253.3 1.8 convolution_convert_fusion.1
  255.1 7.5 %convolution_bitcast_fusion = f32[1280,128]{0,1:T(8,128)} fusion(bf16[2048,1280]{1,0:T(8,128)(2,1)} %param.6, bf16[128,1280]{1,0:T(8,128)(2,1)S(1)} %convolution_convert_fusion.1), kind=kOutput, calls=%fused_computation | convolution fusion | flops 1342439424 | bytes 6225920 | tf_op jit(solution)/shard_map/dot_general | solution.py:41
  262.7 128.8 %all-reduce.5.cloned.1.call-done = f32[1280,128]{0,1:T(8,128)} async-done(((f32[1280,128]{0,1:T(8,128)}), f32[1280,128]{0,1:T(8,128)}) %all-reduce.5.cloned.1.call-update) | async-done | bytes 655376 | tf_op jit(solution)/shard_map/psum | solution.py:44
  391.4 2.0 fusion.5
  393.6 11.9 %cholesky.81 = f32[128,128]{1,0:T(8,128)S(1)} custom-call(f32[128,128]{1,0:T(8,128)S(1)} %fusion.21), custom_call_target="Cholesky" | custom-call | tf_op jit(solution)/shard_map/jit(cholesky)/cholesky | solution.py:18
  405.5 0.6 compare_reduce_fusion
  406.2 0.7 fusion.31
  406.8 9.8 %custom-call.9 = f32[1,128,128]{1,2,0:T(8,128)S(1)} custom-call(f32[1,128,128]{2,1,0:T(8,128)S(1)} %get-tuple-element.9), custom_call_target="InvertDiagBlocksLowerTriangular" | custom-call | tf_op jit(solution)/shard_map/jit(_solve_triangular)/triangular_solve | solution.py:19
  416.6 0.7 copy.14
  417.4 2.3 fusion
  419.7 0.6 dynamic-slice_bitcast_fusion
  (16 shorter events, 0.5 us)
Async XLA Ops:
  7.2 1.0 copy-start
  7.2 22.6 %copy-start.1 = (bf16[1,1024,128]{2,1,0:T(8,128)(2,1)S(1)}, bf16[1,1024,128]{2,1,0:T(8,128)(2,1)}, u32[]{:S(2)}) copy-start(bf16[1,1024,128]{2,1,0:T(8,128)(2,1)} %param.8) | copy-start | bytes 786436
  7.2 221.1 %all-reduce.3.cloned.1.call-start = ((), (), s32[]{:S(2)}) async-start(), calls=%async_computation.1 | async-start | bytes 1310720 | tf_op jit(solution)/shard_map/psum | solution.py:44
  100.4 291.0 %all-reduce.5.cloned.1.call-start = ((), (), s32[]{:S(2)}) async-start(), calls=%async_computation.2 | async-start | bytes 1310720 | tf_op jit(solution)/shard_map/psum | solution.py:44
Sparse Core Ops, SparseCore 0:
  100.6 127.7 all-reduce.2
  262.8 128.6 all-reduce.4

commit v2 on v0

--- a/solution.py
+++ b/solution.py
@@ -1,9 +1,19 @@
+import functools
 import jax
 import jax.numpy as jnp
 from jax import lax
 from jax.sharding import PartitionSpec as P
 
 ITERS = 2
+
+
+def guide_the_slot(u_in, peer_axis, axis_tag):
+    for it in (peer_axis, axis_tag):
+        u_in = jax.lax.psum(u_in, it)
+    return u_in
+
+
+cut_the_notes = functools.partial(guide_the_slot, peer_axis="rep", axis_tag="dp")
 
 
 def whole_factor(matrix):
@@ -36,7 +46,7 @@
         local_sum = lax.dot_general(
             tokens, projected, (((0,), (0,)), ((), ())), preferred_element_type=jnp.float32
         )
-        summed = lax.psum(local_sum, ("dp", "rep"))
+        summed = cut_the_notes(local_sum)
         current, factor = whole_factor(summed / total_tokens)
     owned = lax.dynamic_slice_in_dim(current, lax.axis_index("dp") * strip, strip, 0)
     return (owned, factor)

time: 454 us -> 417 us (0.919)
  waiting for transfers between devices: 288 us -> 252 us
    psum x2 -> x4, waiting for transfers between devices: 260 us -> 223 us  [guide_the_slot(): u_in = jax.lax.psum(u_in, it)]
  transfers between devices with their start and end apart: 3 -> 5, of which waited for: 3 -> 5; matrix products, arithmetic and copies ran while one was open for 0% -> 0% of each run, Pallas kernels for 0% -> 0%
where the time goes in v2:
time: 417 us
  waiting for transfers between devices  252 us (60%)
  other arithmetic  68.6 us (16%)
  blocking collectives  50 us (12%)
  matrix products  29.4 us (7%)
  between operations  13.9 us (3%)
    psum x4, waiting for transfers between devices, guide_the_slot(): u_in = jax.lax.psum(u_in, it)  223 us
    another operation x9, other arithmetic, whole_factor(): lower = jnp.linalg.cholesky(gram)  37.2 us
    all_gather x1, blocking collectives, body(): gathered = lax.all_gather(start, 'dp', axis=0, tiled=True)  32 us
    another operation x5, other arithmetic, whole_factor(): jax.scipy.linalg.solve_triangular(lower, matrix.T, lower=True)  30.7 us
    psum x1, waiting for transfers between devices, body(): start = lax.psum(local_start, 'rep')  28.8 us
    all_to_all x1, blocking collectives, body(): lax.all_to_all(sketch, 'dp', split_axis=1, concat_axis=0, tiled=True)  18 us
    dot_general x2, matrix products, body(): lax.dot_general(tokens, projected, (((0,), (0,)), ((), ())), preferred_el...  15 us
  transfers between devices with their start and end apart: 5, of which 5 were waited for; matrix products, arithmetic and copies ran while one was open for 0% of the time, Pallas kernels for 0%

profile of v2, /device:TPU:0, one launch (start us, length us, event | category | flops | bytes accessed | tf_op | source)
XLA Modules:
  0.0 416.9 jit_solution(11257115136856673982)
XLA Ops:
  7.2 1.0 copy-done
  8.2 3.4 convolution_convert_fusion.4
  11.8 18.0 %all_to_all.19 = bf16[128,8,160]{0,2,1:T(8,128)(2,1)S(1)} all-to-all(bf16[128,8,160]{0,2,1:T(8,128)(2,1)S(1)} %bitcast.66), channel_id=1, replica_groups=mesh['dp'=8,'rep'=4] {'dp'}, dimensions={1} | all-to-all | bytes 655360 | tf_op jit(solution)/shard_map/all_to_all | solution.py:34
  29.8 0.9 fusion.10
  30.7 28.8 %all-reduce.6.cloned.1.call-done = f32[160,128]{1,0:T(8,128)} async-done(((f32[160,128]{1,0:T(8,128)}), f32[160,128]{1,0:T(8,128)}) %all-reduce.6.cloned.1.call-update) | async-done | bytes 81936 | tf_op jit(solution)/shard_map/psum | solution.py:38
  59.5 32.0 %all_gather.3 = f32[1280,128]{1,0:T(8,128)S(1)} all-gather(f32[160,128]{1,0:T(8,128)} %all-reduce.6.cloned.1.call-done), channel_id=1, replica_groups=mesh['dp'=8,'rep'=4] {'dp'}, dimensions={0}, use_global_device_ids=true | all-gather | bytes 737280 | tf_op jit(solution)/shard_map/all_gather | solution.py:39
  91.5 1.2 fusion.36
  92.8 11.7 %cholesky.59 = f32[128,128]{1,0:T(8,128)S(1)} custom-call(f32[128,128]{1,0:T(8,128)S(1)} %fusion.25), custom_call_target="Cholesky" | custom-call | tf_op jit(solution)/shard_map/jit(cholesky)/cholesky | solution.py:23
  104.6 0.6 compare_reduce_fusion.2
  105.2 0.7 fusion.18
  105.9 9.8 %custom-call.7 = f32[1,128,128]{1,2,0:T(8,128)S(1)} custom-call(f32[1,128,128]{2,1,0:T(8,128)S(1)} %fusion.18), custom_call_target="InvertDiagBlocksLowerTriangular" | custom-call | tf_op jit(solution)/shard_map/jit(_solve_triangular)/triangular_solve | solution.py:24
  115.7 0.8 convolution_convert_fusion.3
  116.5 7.5 %convolution_bitcast_fusion.1 = f32[1280,128]{0,1:T(8,128)} fusion(bf16[2048,1280]{1,0:T(8,128)(2,1)} %param.6, bf16[128,1280]{1,0:T(8,128)(2,1)S(1)} %convolution_convert_fusion.3), kind=kOutput, calls=%fused_computation.1 | convolution fusion | flops 1342439424 | bytes 6225920 | tf_op jit(solution)/shard_map/dot_general | solution.py:46
  124.1 35.4 %all-reduce.8.cloned.1.call-done = f32[1280,128]{0,1:T(8,128)} async-done(((f32[1280,128]{0,1:T(8,128)}), f32[1280,128]{0,1:T(8,128)}) %all-reduce.8.cloned.1.call-update) | async-done | bytes 655376 | tf_op jit(solution)/shard_map/psum | solution.py:12
  159.7 76.9 %all-reduce.10.cloned.1.call-done = f32[1280,128]{0,1:T(8,128)} async-done(((f32[1280,128]{0,1:T(8,128)}), f32[1280,128]{0,1:T(8,128)}) %all-reduce.10.cloned.1.call-update) | async-done | bytes 655376 | tf_op jit(solution)/shard_map/psum | solution.py:12
  236.6 2.0 fusion.8
  238.8 11.7 %cholesky.70 = f32[128,128]{1,0:T(8,128)S(1)} custom-call(f32[128,128]{1,0:T(8,128)S(1)} %fusion.23), custom_call_target="Cholesky" | custom-call | tf_op jit(solution)/shard_map/jit(cholesky)/cholesky | solution.py:23
  250.5 0.6 compare_reduce_fusion.1
  251.2 0.7 fusion.19
  251.8 9.8 %custom-call.8 = f32[1,128,128]{1,2,0:T(8,128)S(1)} custom-call(f32[1,128,128]{2,1,0:T(8,128)S(1)} %fusion.19), custom_call_target="InvertDiagBlocksLowerTriangular" | custom-call | tf_op jit(solution)/shard_map/jit(_solve_triangular)/triangular_solve | solution.py:24
  261.7 1.8 convolution_convert_fusion.1
  263.5 7.5 %convolution_bitcast_fusion = f32[1280,128]{0,1:T(8,128)} fusion(bf16[2048,1280]{1,0:T(8,128)(2,1)} %param.6, bf16[128,1280]{1,0:T(8,128)(2,1)S(1)} %convolution_convert_fusion.1), kind=kOutput, calls=%fused_computation | convolution fusion | flops 1342439424 | bytes 6225920 | tf_op jit(solution)/shard_map/dot_general | solution.py:46
  271.3 33.4 %all-reduce.12.cloned.1.call-done = f32[1280,128]{0,1:T(8,128)} async-done(((f32[1280,128]{0,1:T(8,128)}), f32[1280,128]{0,1:T(8,128)}) %all-reduce.12.cloned.1.call-update) | async-done | bytes 655376 | tf_op jit(solution)/shard_map/psum | solution.py:12
  304.7 77.0 %all-reduce.14.cloned.1.call-done = f32[1280,128]{0,1:T(8,128)} async-done(((f32[1280,128]{0,1:T(8,128)}), f32[1280,128]{0,1:T(8,128)}) %all-reduce.14.cloned.1.call-update) | async-done | bytes 655376 | tf_op jit(solution)/shard_map/psum | solution.py:12
  381.7 2.0 fusion.5
  383.8 11.7 %cholesky.81 = f32[128,128]{1,0:T(8,128)S(1)} custom-call(f32[128,128]{1,0:T(8,128)S(1)} %fusion.21), custom_call_target="Cholesky" | custom-call | tf_op jit(solution)/shard_map/jit(cholesky)/cholesky | solution.py:23
  395.6 0.6 compare_reduce_fusion
  396.2 0.7 fusion.31
  396.9 9.8 %custom-call.9 = f32[1,128,128]{1,2,0:T(8,128)S(1)} custom-call(f32[1,128,128]{2,1,0:T(8,128)S(1)} %get-tuple-element.9), custom_call_target="InvertDiagBlocksLowerTriangular" | custom-call | tf_op jit(solution)/shard_map/jit(_solve_triangular)/triangular_solve | solution.py:24
  406.7 0.7 copy.14
  407.4 2.3 fusion
  409.7 0.6 dynamic-slice_bitcast_fusion
  (23 shorter events, 1.3 us)
Async XLA Ops:
  7.2 1.0 copy-start
  7.2 22.6 %copy-start.1 = (bf16[1,1024,128]{2,1,0:T(8,128)(2,1)S(1)}, bf16[1,1024,128]{2,1,0:T(8,128)(2,1)}, u32[]{:S(2)}) copy-start(bf16[1,1024,128]{2,1,0:T(8,128)(2,1)} %param.8) | copy-start | bytes 786436
  7.2 52.3 %all-reduce.6.cloned.1.call-start = ((), (), s32[]{:S(2)}) async-start(), calls=%async_computation.1 | async-start | bytes 163840 | tf_op jit(solution)/shard_map/psum | solution.py:38
  30.7 128.8 %all-reduce.8.cloned.1.call-start = ((), (), s32[]{:S(2)}) async-start(), calls=%async_computation.2 | async-start | bytes 1310720 | tf_op jit(solution)/shard_map/psum | solution.py:12
  124.0 112.6 %all-reduce.10.cloned.1.call-start = ((), (), s32[]{:S(2)}) async-start(), calls=%async_computation.3 | async-start | bytes 1310720 | tf_op jit(solution)/shard_map/psum | solution.py:12
  159.5 145.2 %all-reduce.12.cloned.1.call-start = ((), (), s32[]{:S(2)}) async-start(), calls=%async_computation.4 | async-start | bytes 1310720 | tf_op jit(solution)/shard_map/psum | solution.py:12
  271.0 110.6 %all-reduce.14.cloned.1.call-start = ((), (), s32[]{:S(2)}) async-start(), calls=%async_computation.5 | async-start | bytes 1310720 | tf_op jit(solution)/shard_map/psum | solution.py:12
Sparse Core Ops, SparseCore 0:
  30.8 28.6 all-reduce.5
  124.1 35.2 all-reduce.7
  162.9 73.6 all-reduce.9
  271.1 33.4 all-reduce.11
  308.0 73.6 all-reduce.13
